TPU v7x, 32 devices: a whole 2x2x4 slice. The times are simulated.
32 devices in a mesh: wide: 8 (over y, x, core), narrow: 4 (over z).
Axes of the slice: x: 2, y: 2, z: 4, core: 2. Of those that a mesh axis runs over, the one named last changes fastest.
Arguments:
- schur_matrix: bfloat16 [8, 4, 3, 1024, 1024], P('wide', 'narrow')
- face_inverse: bfloat16 [8, 4, 3, 8, 128, 128], P('wide', 'narrow')
- deluxe: bfloat16 [8, 4, 3, 8, 128, 128], P('wide', 'narrow')
- primal_weight: float32 [8, 4, 3, 8, 128], P('wide', 'narrow'), may hold values from 0.05 to 0.3
- coarse_group: float32 [8, 96, 96], P('wide', 'narrow')
- coarse_map: float32 [8, 96, 8], P('wide', 'narrow'), may hold values from -0.625 to 0.625
- coarse_top: float32 [64, 64], P('wide')
- load_vector: bfloat16 [8, 4, 3, 8, 128, 128], P('wide', 'narrow'), may hold values from -6 to 6
- previous: bfloat16 [8, 4, 3, 8, 128, 128], P('wide', 'narrow'), may hold values from -3 to 3
- slot_count: int32 [8, 4], P('wide', 'narrow'), may hold values from 1 to 3, as said below
- partner: int32 [8, 4, 3, 8], P('wide', 'narrow'), may hold values from -1 to 2, as said below
- face_size: int32 [8, 4, 3, 8], P('wide', 'narrow'), may hold values from 0 to 128, as said below
Outputs:
- solution: float32 [8, 4, 3, 8, 128, 128], P('wide', 'narrow')
- residual: float32 [8, 4, 3, 8, 128, 128], P('wide', 'narrow')
Inputs may be any that keep to these rules, and one draw needn't show every extreme that they name: Slots of a device below its slot_count hold subdomains; the others are empty. `face_size`: both sides of a face with a partner have the same size; faces of empty slots have size 0, all other faces at least 32.
All inputs are finite; a program needn't handle non-finite values.
Results may differ from a plain program's by a relative error of at most 0.00355.
The roundings to bfloat16 on the way count: a program that leaves them out, or rounds other values in their place, can miss the bound.
Values may be sent and summed in bfloat16 or wider, within the bound.
No kernel may reach another device: no remote copies, remote signals or barrier semaphores. Data moves between devices by JAX's collectives and lax.ppermute only.
A program may use at most 128 MiB of HBM per device.

v0:
```python
import jax
import jax.numpy as jnp
from jax import lax
from jax.sharding import PartitionSpec as P

ITERS = 2
precise = lax.Precision.HIGHEST


def with_halo(block, sides, width, periodic):
    for axis, dim in sides:
        count = lax.axis_size(axis)
        forward = [(i, i + 1) for i in range(count - 1)]
        if periodic:
            forward.append((count - 1, 0))
        backward = [(target, source) for source, target in forward]
        low = lax.ppermute(
            lax.slice_in_dim(block, block.shape[dim] - width, None, axis=dim), axis, forward
        )
        high = lax.ppermute(lax.slice_in_dim(block, 0, width, axis=dim), axis, backward)
        block = jnp.concatenate([low, block, high], axis=dim)
    return block


def pick_partner(sources, partner):
    slot_total = sources.shape[1]
    chosen = partner[:, :, None] == jnp.arange(slot_total, dtype=jnp.int32)[None, None, :]
    spread = jnp.where(chosen[:, :, :, None, None], sources[None], jnp.zeros((), sources.dtype))
    return jnp.sum(spread, axis=2)


def face_sources(values, wide_got, narrow_got):
    return jnp.stack(
        [
            narrow_got[0],
            narrow_got[3],
            wide_got[0],
            wide_got[3],
            values[:, 5],
            values[:, 4],
            values[:, 7],
            values[:, 6],
        ],
        axis=0,
    )


def partner_full(values, partner):
    wide_got = with_halo(jnp.stack([values[:, 2], values[:, 3]], axis=0), (("wide", 0),), 1, True)
    narrow_got = with_halo(
        jnp.stack([values[:, 0], values[:, 1]], axis=0), (("narrow", 0),), 1, False
    )
    return pick_partner(face_sources(values, wide_got, narrow_got), partner)


def partner_half(values, partner):
    wide_got = with_halo(jnp.stack([values[:, 2], values[:, 3]], axis=0), (("wide", 0),), 1, True)
    narrow_got = with_halo(
        jnp.stack([values[:, 0], values[:, 1]], axis=0), (("narrow", 0),), 1, False
    )
    return pick_partner(face_sources(values, wide_got, narrow_got), partner)


def body(
    schur_matrix,
    face_inverse,
    deluxe,
    primal_weight,
    coarse_group,
    coarse_map,
    coarse_top,
    load_vector,
    previous,
    slot_count,
    partner,
    face_size,
):
    schur_matrix = schur_matrix[0, 0]
    face_inverse = face_inverse[0, 0]
    deluxe = deluxe[0, 0]
    primal_weight = primal_weight[0, 0]
    coarse_group = coarse_group[0]
    coarse_map = coarse_map[0]
    load_vector = load_vector[0, 0]
    previous = previous[0, 0]
    live_count = slot_count[0, 0]
    partner = partner[0, 0]
    face_size = face_size[0, 0]
    slot_total, face_total, face_width, columns = load_vector.shape
    block_order = schur_matrix.shape[1]
    slot_alive = jnp.arange(slot_total, dtype=jnp.int32)[:, None, None] < live_count
    inside = jnp.arange(face_width, dtype=jnp.int32)[None, None, :] < face_size[:, :, None]
    live_mask = jnp.where(jnp.logical_and(slot_alive, inside), 1.0, 0.0).astype(jnp.float32)[
        ..., None
    ]
    linked = (partner >= 0)[:, :, None, None]

    def global_inner(first_vec, second_vec, weights):
        return lax.psum(
            jnp.sum(weights * first_vec * second_vec, axis=(0, 1, 2)), ("wide", "narrow")
        )

    def operator(values):
        direction_half = values.astype(jnp.bfloat16)
        stacked = direction_half.reshape(slot_total, block_order, columns)
        result = jnp.einsum(
            "sij,sjr->sir", schur_matrix, stacked, preferred_element_type=jnp.float32
        )
        return live_mask * result.reshape(values.shape)

    def precondition(values):
        res_half = values.astype(jnp.bfloat16)
        scaled = live_mask * jnp.einsum(
            "sfkj,sfkr->sfjr", deluxe, res_half, preferred_element_type=jnp.float32
        )
        scaled_half = scaled.astype(jnp.bfloat16)
        local_part = jnp.einsum(
            "sfjk,sfkr->sfjr", face_inverse, scaled_half, preferred_element_type=jnp.float32
        )
        coarse_in = jnp.sum(primal_weight[..., None] * scaled, axis=2).reshape(
            slot_total * face_total, columns
        )
        group_vec = lax.all_gather(coarse_in, "narrow", axis=0, tiled=True)
        group_part = jnp.dot(coarse_group, group_vec, precision=precise)
        restricted = lax.psum(jnp.dot(coarse_map.T, coarse_in, precision=precise), "narrow")
        everyone = lax.all_gather(restricted, "wide", axis=0, tiled=True)
        top_part = jnp.dot(coarse_top, everyone, precision=precise)
        coarse_out = group_part + jnp.dot(coarse_map, top_part, precision=precise)
        correction = local_part + primal_weight[..., None] * coarse_out.reshape(
            slot_total, face_total, 1, columns
        )
        corr_half = (live_mask * correction).astype(jnp.bfloat16)
        weighted = live_mask * jnp.einsum(
            "sfjk,sfkr->sfjr", deluxe, corr_half, preferred_element_type=jnp.float32
        )
        assembled = weighted + partner_full(weighted, partner)
        return (assembled, weighted)

    def norm_of(values, weighted):
        return global_inner(values, weighted, 1.0)

    prev_full = previous.astype(jnp.float32)
    prev_partner = partner_half(previous, partner).astype(jnp.float32)
    averaged = live_mask * jnp.where(linked, 0.5 * (prev_full + prev_partner), prev_full)
    start_local = live_mask * load_vector.astype(jnp.float32) - operator(averaged)
    residual = start_local + partner_full(start_local, partner)
    solution = averaged
    precond, weighted = precondition(residual)
    precond_norm = norm_of(residual, weighted)
    direction = precond
    for iteration in range(ITERS):
        image_local = operator(direction)
        curvature = global_inner(direction, image_local, 1.0)
        image_full = image_local + partner_full(image_local, partner)
        step_size = precond_norm / curvature
        solution = solution + step_size * direction
        residual = residual - step_size * image_full
        if iteration + 1 < ITERS:
            precond, weighted = precondition(residual)
            next_norm = norm_of(residual, weighted)
            direction = precond + next_norm / precond_norm * direction
            precond_norm = next_norm
    return (solution[None, None], residual[None, None])


def solution(mesh):
    in_specs = (
        P("wide", "narrow", None, None, None),
        P("wide", "narrow", None, None, None, None),
        P("wide", "narrow", None, None, None, None),
        P("wide", "narrow", None, None, None),
        P("wide", "narrow", None),
        P("wide", "narrow", None),
        P("wide", None),
        P("wide", "narrow", None, None, None, None),
        P("wide", "narrow", None, None, None, None),
        P("wide", "narrow"),
        P("wide", "narrow", None, None),
        P("wide", "narrow", None, None),
    )
    out_specs = (
        P("wide", "narrow", None, None, None, None),
        P("wide", "narrow", None, None, None, None),
    )
    return jax.shard_map(body, mesh=mesh, in_specs=in_specs, out_specs=out_specs, check_vma=False)
```

profile of v0, /device:TPU:0, one launch (start us, length us, event | category | flops | bytes accessed | tf_op | source)
XLA Modules:
  0.0 334.1 jit_solution(3498991599465272584)
XLA Ops:
  1.8 3.4 %collective-permute-start.3 = (bf16[1,3,128,128]{3,2,1,0:T(8,128)(2,1)S(1)}, bf16[1,3,128,128]{3,2,1,0:T(8,128)(2,1)}, u32[]{:S(2)}, u32[]{:S(2)}) collective-permute-start(bf16[1,3,128,128]{3,2,1,0:T(8,128)(2,1)S(1)} %get-tuple-element.33), channel_id=1, source_target_pairs={{4,0},{8,4},{12,8},{16,12},{20,16},{24,20},{28,24},{0,28},{5,1},{9... | collective-permute-start | bytes 294920 | tf_op jit(solution)/shard_map/ppermute | solution.py:20
  6.5 5.2 %collective-permute-start = (bf16[1,3,128,128]{3,2,1,0:T(8,128)(2,1)S(1)}, bf16[1,3,128,128]{3,2,1,0:T(8,128)(2,1)}, u32[]{:S(2)}, u32[]{:S(2)}) collective-permute-start(bf16[1,3,128,128]{3,2,1,0:T(8,128)(2,1)S(1)} %get-tuple-element.36), channel_id=1, source_target_pairs={{0,1},{1,2},{2,3},{4,5},{5,6},{6,7},{8,9},{9,10},{10,11},{12,13},{... | collective-permute-start | bytes 294920 | tf_op jit(solution)/shard_map/ppermute | solution.py:17
  23.3 6.6 %fusion.23 = f32[3,1024,128]{1,2,0:T(8,128)} fusion(bf16[1,1,3,1024,1024]{4,3,2,1,0:T(8,128)(2,1)} %param.12, f32[3,1024,128]{1,2,0:T(8,128)S(1)} %copy.131, f32[3,1024,128]{1,2,0:T(8,128)} %copy.132, f32[3,1024]{1,0:T(4,128)S(1)} %copy-done.29, pred[3,1024]{1,0:T(4,128)(4,1)S(1)} %bitcast.426), kind=kOutput, calls=%fused_computation.50 | convolution fusion | flops 807272448 | bytes 11025408 | tf_op jit(solution)/shard_map/sij,sjr->sir/dot_general | solution.py:106
  39.5 4.6 %collective-permute-done.5 = f32[1,3,128,128]{3,2,1,0:T(8,128)S(1)} collective-permute-done((f32[1,3,128,128]{3,2,1,0:T(8,128)S(1)}, f32[1,3,128,128]{3,2,1,0:T(8,128)S(1)}, u32[]{:S(2)}, u32[]{:S(2)}) %collective-permute-start.5) | collective-permute-done | bytes 196640 | tf_op jit(solution)/shard_map/ppermute | solution.py:20
  49.2 12.1 %psum.42 = f32[8,128]{1,0:T(8,128)S(1)} all-reduce(f32[8,128]{1,0:T(8,128)S(1)} %convolution_bitcast_fusion.1), channel_id=1, replica_groups=mesh['wide'=8,'narrow'=4] {'narrow'}, use_global_device_ids=true, to_apply=%region_3.4 | all-reduce | flops 1024 | bytes 8192 | tf_op jit(solution)/shard_map/psum | solution.py:125
  61.3 8.1 %all_gather.13 = f32[64,128]{1,0:T(8,128)S(1)} all-gather(f32[8,128]{1,0:T(8,128)S(1)} %psum.42), channel_id=1, replica_groups=mesh['wide'=8,'narrow'=4] {'wide'}, dimensions={0}, use_global_device_ids=true | all-gather | bytes 36864 | tf_op jit(solution)/shard_map/all_gather | solution.py:126
  69.4 13.1 %all_gather.12 = f32[96,128]{1,0:T(8,128)S(1)} all-gather(f32[24,128]{1,0:T(8,128)S(1)} %bitcast.423), channel_id=1, replica_groups=mesh['wide'=8,'narrow'=4] {'narrow'}, dimensions={0}, use_global_device_ids=true | all-gather | bytes 61440 | tf_op jit(solution)/shard_map/all_gather | solution.py:123
  90.3 4.5 %collective-permute-done.9 = f32[1,3,128,128]{3,2,1,0:T(8,128)S(1)} collective-permute-done((f32[1,3,128,128]{3,2,1,0:T(8,128)S(1)}, f32[1,3,128,128]{3,2,1,0:T(8,128)S(1)}, u32[]{:S(2)}, u32[]{:S(2)}) %collective-permute-start.9) | collective-permute-done | bytes 196640 | tf_op jit(solution)/shard_map/ppermute | solution.py:20
  99.4 3.4 %fusion.26 = f32[3,1024,128]{1,2,0:T(8,128)} fusion(bf16[3,1024,128]{2,1,0:T(8,128)(2,1)S(1)} %bitcast.416, bf16[1,1,3,1024,1024]{4,3,2,1,0:T(8,128)(2,1)S(1)} %bitcast.400), kind=kOutput, calls=%fused_computation.51 | convolution fusion | flops 805306368 | bytes 8650752 | tf_op jit(solution)/shard_map/sij,sjr->sir/dot_general | solution.py:106
  102.8 3.0 copy.153
  109.8 5.4 %collective-permute-start.12 = (f32[1,3,128,128]{3,2,1,0:T(8,128)}, f32[1,3,128,128]{3,2,1,0:T(8,128)}, u32[]{:S(2)}, u32[]{:S(2)}) collective-permute-start(f32[1,3,128,128]{3,2,1,0:T(8,128)} %get-tuple-element.24), channel_id=1, source_target_pairs={{0,1},{1,2},{2,3},{4,5},{5,6},{6,7},{8,9},{9,10},{10,11},{12,13},{... | collective-permute-start | bytes 589832 | tf_op jit(solution)/shard_map/ppermute | solution.py:17
  117.0 40.9 %all-reduce = (f32[128]{0:T(128)S(1)}, f32[128]{0:T(128)S(1)}) all-reduce(f32[128]{0:T(128)S(1)} %get-tuple-element.20, f32[128]{0:T(128)S(1)} %get-tuple-element.8), channel_id=1, replica_groups=mesh['wide'=8,'narrow'=4] {'wide','narrow'}, use_global_device_ids=true, to_apply=%region_5.6 | all-reduce | flops 256 | bytes 2048 | tf_op jit(solution)/shard_map/psum | solution.py:99
  165.9 10.2 %psum.45 = f32[8,128]{1,0:T(8,128)S(1)} all-reduce(f32[8,128]{1,0:T(8,128)S(1)} %convolution_bitcast_fusion), channel_id=1, replica_groups=mesh['wide'=8,'narrow'=4] {'narrow'}, use_global_device_ids=true, to_apply=%region_11.12 | all-reduce | flops 1024 | bytes 8192 | tf_op jit(solution)/shard_map/psum | solution.py:125
  176.1 9.9 %all_gather.15 = f32[64,128]{1,0:T(8,128)S(1)} all-gather(f32[8,128]{1,0:T(8,128)S(1)} %psum.45), channel_id=1, replica_groups=mesh['wide'=8,'narrow'=4] {'wide'}, dimensions={0}, use_global_device_ids=true | all-gather | bytes 36864 | tf_op jit(solution)/shard_map/all_gather | solution.py:126
  186.1 13.1 %all_gather.14 = f32[96,128]{1,0:T(8,128)S(1)} all-gather(f32[24,128]{1,0:T(8,128)S(1)} %bitcast.422), channel_id=1, replica_groups=mesh['wide'=8,'narrow'=4] {'narrow'}, dimensions={0}, use_global_device_ids=true | all-gather | bytes 61440 | tf_op jit(solution)/shard_map/all_gather | solution.py:123
  199.6 4.4 %multiply_reduce_fusion.1 = (f32[128]{0:T(128)}, f32[3,8,128,128]{3,2,1,0:T(8,128)}) fusion(f32[3,8,128,128]{3,2,1,0:T(8,128)} %copy-done.20, bf16[1,1,3,8,128,128]{5,4,3,2,1,0:T(8,128)(2,1)S(1)} %copy-done.25, f32[3,8,128]{2,1,0:T(8,128)S(1)} %fusion.32, bf16[3,8,128,128]{2,3,1,0:T(8,128)(2,1)S(1)} %get-tuple-element.40, f32[3,8,128]{2,1,0:T(8,128)S(1)} %bitcast.421, ...), kind=kOutput, calls=%fused_computation.39 | convolution fusion | flops 204078976 | bytes 5542400 | tf_op jit(solution)/shard_map/sfjk,sfkr->sfjr/dot_general | solution.py:133
  209.4 40.3 %psum.46 = f32[128]{0:T(128)S(1)} all-reduce(f32[128]{0:T(128)S(1)} %copy-done.38), channel_id=1, replica_groups=mesh['wide'=8,'narrow'=4] {'wide','narrow'}, use_global_device_ids=true, to_apply=%region_13.14 | all-reduce | flops 128 | bytes 1024 | tf_op jit(solution)/shard_map/psum | solution.py:99
  252.6 5.5 %collective-permute-done.18 = f32[1,3,128,128]{3,2,1,0:T(8,128)S(1)} collective-permute-done((f32[1,3,128,128]{3,2,1,0:T(8,128)S(1)}, f32[1,3,128,128]{3,2,1,0:T(8,128)S(1)}, u32[]{:S(2)}, u32[]{:S(2)}) %collective-permute-start.18) | collective-permute-done | bytes 196640 | tf_op jit(solution)/shard_map/ppermute | solution.py:17
  263.1 3.4 %fusion.29 = f32[3,1024,128]{1,2,0:T(8,128)} fusion(bf16[3,1024,128]{2,1,0:T(8,128)(2,1)S(1)} %bitcast.417, bf16[1,1,3,1024,1024]{4,3,2,1,0:T(8,128)(2,1)S(1)} %bitcast.402), kind=kOutput, calls=%fused_computation.52 | convolution fusion | flops 805306368 | bytes 8650752 | tf_op jit(solution)/shard_map/sij,sjr->sir/dot_general | solution.py:106
  269.5 3.2 multiply_reduce_fusion
  272.7 38.1 %psum.47 = f32[128]{0:T(128)S(1)} all-reduce(f32[128]{0:T(128)S(1)} %get-tuple-element.4), channel_id=1, replica_groups=mesh['wide'=8,'narrow'=4] {'wide','narrow'}, use_global_device_ids=true, to_apply=%region_16.17 | all-reduce | flops 128 | bytes 1024 | tf_op jit(solution)/shard_map/psum | solution.py:99
  313.4 4.6 %collective-permute-start.20 = (f32[1,3,128,128]{3,2,1,0:T(8,128)S(1)}, f32[1,3,128,128]{3,2,1,0:T(8,128)S(1)}, u32[]{:S(2)}, u32[]{:S(2)}) collective-permute-start(f32[1,3,128,128]{3,2,1,0:T(8,128)S(1)} %get-tuple-element.15), channel_id=1, source_target_pairs={{0,1},{1,2},{2,3},{4,5},{5,6},{6,7},{8,9},{9,10},{10,11},{12,13},{... | collective-permute-start | bytes 589832 | tf_op jit(solution)/shard_map/ppermute | solution.py:17
  318.1 3.1 fusion.10
  321.8 7.8 %collective-permute-done.22 = f32[1,3,128,128]{3,2,1,0:T(8,128)S(1)} collective-permute-done((f32[1,3,128,128]{3,2,1,0:T(8,128)S(1)}, f32[1,3,128,128]{3,2,1,0:T(8,128)S(1)}, u32[]{:S(2)}, u32[]{:S(2)}) %collective-permute-start.22) | collective-permute-done | bytes 196640 | tf_op jit(solution)/shard_map/ppermute | solution.py:17
  (232 shorter events, 77.9 us)
Async XLA Ops:
  1.8 18.4 %collective-permute-start.3 = (bf16[1,3,128,128]{3,2,1,0:T(8,128)(2,1)S(1)}, bf16[1,3,128,128]{3,2,1,0:T(8,128)(2,1)}, u32[]{:S(2)}, u32[]{:S(2)}) collective-permute-start(bf16[1,3,128,128]{3,2,1,0:T(8,128)(2,1)S(1)} %get-tuple-element.33), channel_id=1, source_target_pairs={{4,0},{8,4},{12,8},{16,12},{20,16},{24,20},{28,24},{0,28},{5,1},{9... | collective-permute-start | bytes 294920 | tf_op jit(solution)/shard_map/ppermute | solution.py:20
  5.2 14.1 %collective-permute-start.2 = (bf16[1,3,128,128]{3,2,1,0:T(8,128)(2,1)S(1)}, bf16[1,3,128,128]{3,2,1,0:T(8,128)(2,1)}, u32[]{:S(2)}, u32[]{:S(2)}) collective-permute-start(bf16[1,3,128,128]{3,2,1,0:T(8,128)(2,1)S(1)} %get-tuple-element.34), channel_id=1, source_target_pairs={{0,4},{4,8},{8,12},{12,16},{16,20},{20,24},{24,28},{28,0},{1,5},{5... | collective-permute-start | bytes 294920 | tf_op jit(solution)/shard_map/ppermute | solution.py:17
  5.2 13.2 %collective-permute-start.1 = (bf16[1,3,128,128]{3,2,1,0:T(8,128)(2,1)S(1)}, bf16[1,3,128,128]{3,2,1,0:T(8,128)(2,1)}, u32[]{:S(2)}, u32[]{:S(2)}) collective-permute-start(bf16[1,3,128,128]{3,2,1,0:T(8,128)(2,1)S(1)} %get-tuple-element.35), channel_id=1, source_target_pairs={{1,0},{2,1},{3,2},{5,4},{6,5},{7,6},{9,8},{10,9},{11,10},{13,12},{... | collective-permute-start | bytes 294920 | tf_op jit(solution)/shard_map/ppermute | solution.py:20
  6.5 11.0 %collective-permute-start = (bf16[1,3,128,128]{3,2,1,0:T(8,128)(2,1)S(1)}, bf16[1,3,128,128]{3,2,1,0:T(8,128)(2,1)}, u32[]{:S(2)}, u32[]{:S(2)}) collective-permute-start(bf16[1,3,128,128]{3,2,1,0:T(8,128)(2,1)S(1)} %get-tuple-element.36), channel_id=1, source_target_pairs={{0,1},{1,2},{2,3},{4,5},{5,6},{6,7},{8,9},{9,10},{10,11},{12,13},{... | collective-permute-start | bytes 294920 | tf_op jit(solution)/shard_map/ppermute | solution.py:17
  33.1 6.4 %collective-permute-start.4 = (f32[1,3,128,128]{3,2,1,0:T(8,128)S(1)}, f32[1,3,128,128]{3,2,1,0:T(8,128)S(1)}, u32[]{:S(2)}, u32[]{:S(2)}) collective-permute-start(f32[1,3,128,128]{3,2,1,0:T(8,128)S(1)} %get-tuple-element.32), channel_id=1, source_target_pairs={{0,1},{1,2},{2,3},{4,5},{5,6},{6,7},{8,9},{9,10},{10,11},{12,13},{... | collective-permute-start | bytes 589832 | tf_op jit(solution)/shard_map/ppermute | solution.py:17
  35.9 8.1 %collective-permute-start.5 = (f32[1,3,128,128]{3,2,1,0:T(8,128)S(1)}, f32[1,3,128,128]{3,2,1,0:T(8,128)S(1)}, u32[]{:S(2)}, u32[]{:S(2)}) collective-permute-start(f32[1,3,128,128]{3,2,1,0:T(8,128)S(1)} %get-tuple-element.31), channel_id=1, source_target_pairs={{1,0},{2,1},{3,2},{5,4},{6,5},{7,6},{9,8},{10,9},{11,10},{13,12},{... | collective-permute-start | bytes 589832 | tf_op jit(solution)/shard_map/ppermute | solution.py:20
  37.2 7.9 %collective-permute-start.7 = (f32[1,3,128,128]{3,2,1,0:T(8,128)S(1)}, f32[1,3,128,128]{3,2,1,0:T(8,128)S(1)}, u32[]{:S(2)}, u32[]{:S(2)}) collective-permute-start(f32[1,3,128,128]{3,2,1,0:T(8,128)S(1)} %get-tuple-element.29), channel_id=1, source_target_pairs={{4,0},{8,4},{12,8},{16,12},{20,16},{24,20},{28,24},{0,28},{5,1},{9... | collective-permute-start | bytes 589832 | tf_op jit(solution)/shard_map/ppermute | solution.py:20
  39.1 6.0 %collective-permute-start.6 = (f32[1,3,128,128]{3,2,1,0:T(8,128)S(1)}, f32[1,3,128,128]{3,2,1,0:T(8,128)S(1)}, u32[]{:S(2)}, u32[]{:S(2)}) collective-permute-start(f32[1,3,128,128]{3,2,1,0:T(8,128)S(1)} %get-tuple-element.30), channel_id=1, source_target_pairs={{0,4},{4,8},{8,12},{12,16},{16,20},{20,24},{24,28},{28,0},{1,5},{5... | collective-permute-start | bytes 589832 | tf_op jit(solution)/shard_map/ppermute | solution.py:17
  85.5 4.7 %collective-permute-start.8 = (f32[1,3,128,128]{3,2,1,0:T(8,128)S(1)}, f32[1,3,128,128]{3,2,1,0:T(8,128)S(1)}, u32[]{:S(2)}, u32[]{:S(2)}) collective-permute-start(f32[1,3,128,128]{3,2,1,0:T(8,128)S(1)} %get-tuple-element.28), channel_id=1, source_target_pairs={{0,1},{1,2},{2,3},{4,5},{5,6},{6,7},{8,9},{9,10},{10,11},{12,13},{... | collective-permute-start | bytes 589832 | tf_op jit(solution)/shard_map/ppermute | solution.py:17
  87.1 7.7 %collective-permute-start.9 = (f32[1,3,128,128]{3,2,1,0:T(8,128)S(1)}, f32[1,3,128,128]{3,2,1,0:T(8,128)S(1)}, u32[]{:S(2)}, u32[]{:S(2)}) collective-permute-start(f32[1,3,128,128]{3,2,1,0:T(8,128)S(1)} %get-tuple-element.27), channel_id=1, source_target_pairs={{1,0},{2,1},{3,2},{5,4},{6,5},{7,6},{9,8},{10,9},{11,10},{13,12},{... | collective-permute-start | bytes 589832 | tf_op jit(solution)/shard_map/ppermute | solution.py:20
  88.5 7.3 %collective-permute-start.11 = (f32[1,3,128,128]{3,2,1,0:T(8,128)S(1)}, f32[1,3,128,128]{3,2,1,0:T(8,128)S(1)}, u32[]{:S(2)}, u32[]{:S(2)}) collective-permute-start(f32[1,3,128,128]{3,2,1,0:T(8,128)S(1)} %get-tuple-element.25), channel_id=1, source_target_pairs={{4,0},{8,4},{12,8},{16,12},{20,16},{24,20},{28,24},{0,28},{5,1},{9... | collective-permute-start | bytes 589832 | tf_op jit(solution)/shard_map/ppermute | solution.py:20
  88.6 7.2 %collective-permute-start.10 = (f32[1,3,128,128]{3,2,1,0:T(8,128)S(1)}, f32[1,3,128,128]{3,2,1,0:T(8,128)S(1)}, u32[]{:S(2)}, u32[]{:S(2)}) collective-permute-start(f32[1,3,128,128]{3,2,1,0:T(8,128)S(1)} %get-tuple-element.26), channel_id=1, source_target_pairs={{0,4},{4,8},{8,12},{12,16},{16,20},{20,24},{24,28},{28,0},{1,5},{5... | collective-permute-start | bytes 589832 | tf_op jit(solution)/shard_map/ppermute | solution.py:17
  109.8 48.2 %collective-permute-start.12 = (f32[1,3,128,128]{3,2,1,0:T(8,128)}, f32[1,3,128,128]{3,2,1,0:T(8,128)}, u32[]{:S(2)}, u32[]{:S(2)}) collective-permute-start(f32[1,3,128,128]{3,2,1,0:T(8,128)} %get-tuple-element.24), channel_id=1, source_target_pairs={{0,1},{1,2},{2,3},{4,5},{5,6},{6,7},{8,9},{9,10},{10,11},{12,13},{... | collective-permute-start | bytes 589832 | tf_op jit(solution)/shard_map/ppermute | solution.py:17
  115.2 43.8 %collective-permute-start.13 = (f32[1,3,128,128]{3,2,1,0:T(8,128)}, f32[1,3,128,128]{3,2,1,0:T(8,128)}, u32[]{:S(2)}, u32[]{:S(2)}) collective-permute-start(f32[1,3,128,128]{3,2,1,0:T(8,128)} %get-tuple-element.23), channel_id=1, source_target_pairs={{1,0},{2,1},{3,2},{5,4},{6,5},{7,6},{9,8},{10,9},{11,10},{13,12},{... | collective-permute-start | bytes 589832 | tf_op jit(solution)/shard_map/ppermute | solution.py:20
  116.4 44.4 %collective-permute-start.15 = (f32[1,3,128,128]{3,2,1,0:T(8,128)S(1)}, f32[1,3,128,128]{3,2,1,0:T(8,128)}, u32[]{:S(2)}, u32[]{:S(2)}) collective-permute-start(f32[1,3,128,128]{3,2,1,0:T(8,128)S(1)} %get-tuple-element.21), channel_id=1, source_target_pairs={{4,0},{8,4},{12,8},{16,12},{20,16},{24,20},{28,24},{0,28},{5,1},{9... | collective-permute-start | bytes 589832 | tf_op jit(solution)/shard_map/ppermute | solution.py:20
  116.5 43.4 %collective-permute-start.14 = (f32[1,3,128,128]{3,2,1,0:T(8,128)}, f32[1,3,128,128]{3,2,1,0:T(8,128)}, u32[]{:S(2)}, u32[]{:S(2)}) collective-permute-start(f32[1,3,128,128]{3,2,1,0:T(8,128)} %get-tuple-element.22), channel_id=1, source_target_pairs={{0,4},{4,8},{8,12},{12,16},{16,20},{20,24},{24,28},{28,0},{1,5},{5... | collective-permute-start | bytes 589832 | tf_op jit(solution)/shard_map/ppermute | solution.py:17
  206.1 44.6 %collective-permute-start.16 = (f32[1,3,128,128]{3,2,1,0:T(8,128)}, f32[1,3,128,128]{3,2,1,0:T(8,128)}, u32[]{:S(2)}, u32[]{:S(2)}) collective-permute-start(f32[1,3,128,128]{3,2,1,0:T(8,128)} %get-tuple-element.19), channel_id=1, source_target_pairs={{0,1},{1,2},{2,3},{4,5},{5,6},{6,7},{8,9},{9,10},{10,11},{12,13},{... | collective-permute-start | bytes 589832 | tf_op jit(solution)/shard_map/ppermute | solution.py:17
  208.1 43.6 %collective-permute-start.17 = (f32[1,3,128,128]{3,2,1,0:T(8,128)S(1)}, f32[1,3,128,128]{3,2,1,0:T(8,128)}, u32[]{:S(2)}, u32[]{:S(2)}) collective-permute-start(f32[1,3,128,128]{3,2,1,0:T(8,128)S(1)} %get-tuple-element.18), channel_id=1, source_target_pairs={{1,0},{2,1},{3,2},{5,4},{6,5},{7,6},{9,8},{10,9},{11,10},{13,12},{... | collective-permute-start | bytes 589832 | tf_op jit(solution)/shard_map/ppermute | solution.py:20
  249.8 8.4 %collective-permute-start.19 = (f32[1,3,128,128]{3,2,1,0:T(8,128)S(1)}, f32[1,3,128,128]{3,2,1,0:T(8,128)S(1)}, u32[]{:S(2)}, u32[]{:S(2)}) collective-permute-start(f32[1,3,128,128]{3,2,1,0:T(8,128)S(1)} %get-tuple-element.16), channel_id=1, source_target_pairs={{4,0},{8,4},{12,8},{16,12},{20,16},{24,20},{28,24},{0,28},{5,1},{9... | collective-permute-start | bytes 589832 | tf_op jit(solution)/shard_map/ppermute | solution.py:20
  250.7 7.4 %collective-permute-start.18 = (f32[1,3,128,128]{3,2,1,0:T(8,128)S(1)}, f32[1,3,128,128]{3,2,1,0:T(8,128)S(1)}, u32[]{:S(2)}, u32[]{:S(2)}) collective-permute-start(f32[1,3,128,128]{3,2,1,0:T(8,128)S(1)} %get-tuple-element.17), channel_id=1, source_target_pairs={{0,4},{4,8},{8,12},{12,16},{16,20},{20,24},{24,28},{28,0},{1,5},{5... | collective-permute-start | bytes 589832 | tf_op jit(solution)/shard_map/ppermute | solution.py:17
  312.1 9.6 %collective-permute-start.21 = (f32[1,3,128,128]{3,2,1,0:T(8,128)S(1)}, f32[1,3,128,128]{3,2,1,0:T(8,128)S(1)}, u32[]{:S(2)}, u32[]{:S(2)}) collective-permute-start(f32[1,3,128,128]{3,2,1,0:T(8,128)S(1)} %get-tuple-element.14), channel_id=1, source_target_pairs={{1,0},{2,1},{3,2},{5,4},{6,5},{7,6},{9,8},{10,9},{11,10},{13,12},{... | collective-permute-start | bytes 589832 | tf_op jit(solution)/shard_map/ppermute | solution.py:20
  313.4 8.3 %collective-permute-start.20 = (f32[1,3,128,128]{3,2,1,0:T(8,128)S(1)}, f32[1,3,128,128]{3,2,1,0:T(8,128)S(1)}, u32[]{:S(2)}, u32[]{:S(2)}) collective-permute-start(f32[1,3,128,128]{3,2,1,0:T(8,128)S(1)} %get-tuple-element.15), channel_id=1, source_target_pairs={{0,1},{1,2},{2,3},{4,5},{5,6},{6,7},{8,9},{9,10},{10,11},{12,13},{... | collective-permute-start | bytes 589832 | tf_op jit(solution)/shard_map/ppermute | solution.py:17
  321.2 8.3 %collective-permute-start.23 = (f32[1,3,128,128]{3,2,1,0:T(8,128)S(1)}, f32[1,3,128,128]{3,2,1,0:T(8,128)S(1)}, u32[]{:S(2)}, u32[]{:S(2)}) collective-permute-start(f32[1,3,128,128]{3,2,1,0:T(8,128)S(1)} %get-tuple-element.12), channel_id=1, source_target_pairs={{4,0},{8,4},{12,8},{16,12},{20,16},{24,20},{28,24},{0,28},{5,1},{9... | collective-permute-start | bytes 589832 | tf_op jit(solution)/shard_map/ppermute | solution.py:20
  321.5 8.0 %collective-permute-start.22 = (f32[1,3,128,128]{3,2,1,0:T(8,128)S(1)}, f32[1,3,128,128]{3,2,1,0:T(8,128)S(1)}, u32[]{:S(2)}, u32[]{:S(2)}) collective-permute-start(f32[1,3,128,128]{3,2,1,0:T(8,128)S(1)} %get-tuple-element.13), channel_id=1, source_target_pairs={{0,4},{4,8},{8,12},{12,16},{16,20},{20,24},{24,28},{28,0},{1,5},{5... | collective-permute-start | bytes 589832 | tf_op jit(solution)/shard_map/ppermute | solution.py:17
  (47 other events, 689.4 us)
where the time goes:
time: 336 us; the launch traced here: 334 us
  blocking collectives  186 us (55%)
  local copies, waits for them, and re-layouts  38.2 us (11%)
  starting transfers between devices  37.2 us (11%)
  waiting for transfers between devices  25.9 us (8%)
  matrix products  24.9 us (7%)
  other arithmetic  19.7 us (6%)
    psum x3, blocking collectives, global_inner(): lax.psum(jnp.sum(weights * first_vec * second_vec, axis=(0, 1, 2)), ('wid...  119 us
    all_gather x2, blocking collectives, precondition(): group_vec = lax.all_gather(coarse_in, 'narrow', axis=0, tiled=True)  26.2 us
    unnamed x141, local copies, waits for them, and re-layouts  23 us
    ppermute x12, starting transfers between devices, with_halo(): lax.ppermute(lax.slice_in_dim(block, block.shape[dim] - width, None, axis...  22.7 us
    psum x2, blocking collectives, precondition(): lax.psum(jnp.dot(coarse_map.T, coarse_in, precision=precise), 'narrow')  22.3 us
    all_gather x2, blocking collectives, precondition(): everyone = lax.all_gather(restricted, 'wide', axis=0, tiled=True)  18 us
    ppermute x12, waiting for transfers between devices, with_halo(): lax.ppermute(lax.slice_in_dim(block, block.shape[dim] - width, None, axis...  16.8 us
    ppermute x12, starting transfers between devices, with_halo(): lax.ppermute(lax.slice_in_dim(block, 0, width, axis=dim), axis, backward)  14.5 us
  transfers between devices with their start and end apart: 24, of which 8 were waited for; matrix products, arithmetic and copies ran while one was open for 5% of the time, Pallas kernels for 0%

commit v1 on v0

--- a/solution.py
+++ b/solution.py
@@ -122,7 +122,9 @@
         )
         group_vec = lax.all_gather(coarse_in, "narrow", axis=0, tiled=True)
         group_part = jnp.dot(coarse_group, group_vec, precision=precise)
-        restricted = lax.psum(jnp.dot(coarse_map.T, coarse_in, precision=precise), "narrow")
+        restricted = jnp.sum(
+            lax.all_gather(jnp.dot(coarse_map.T, coarse_in, precision=precise), "narrow"), axis=0
+        )
         everyone = lax.all_gather(restricted, "wide", axis=0, tiled=True)
         top_part = jnp.dot(coarse_top, everyone, precision=precise)
         coarse_out = group_part + jnp.dot(coarse_map, top_part, precision=precise)

time: 336 us -> 344 us (1.024)
  blocking collectives: 186 us -> 193 us
    all_gather x0 -> x2, blocking collectives: none -> 28.1 us  [precondition(): lax.all_gather(jnp.dot(coarse_map.T, coarse_in, precision=precise), 'narr...]
    psum x2 -> x0, blocking collectives: 22.3 us -> none  [precondition(): lax.psum(jnp.dot(coarse_map.T, coarse_in, precision=precise), 'narrow')]
where the time goes in v1:
time: 344 us; the launch traced here: 343 us
  blocking collectives  193 us (56%)
  starting transfers between devices  38.4 us (11%)
  local copies, waits for them, and re-layouts  38.2 us (11%)
  waiting for transfers between devices  26.3 us (8%)
  matrix products  25.3 us (7%)
  other arithmetic  19.7 us (6%)
    psum x3, blocking collectives, global_inner(): lax.psum(jnp.sum(weights * first_vec * second_vec, axis=(0, 1, 2)), ('wid...  121 us
    all_gather x2, blocking collectives, precondition(): lax.all_gather(jnp.dot(coarse_map.T, coarse_in, precision=precise), 'narr...  28.1 us
    all_gather x2, blocking collectives, precondition(): group_vec = lax.all_gather(coarse_in, 'narrow', axis=0, tiled=True)  26.1 us
    ppermute x12, starting transfers between devices, with_halo(): lax.ppermute(lax.slice_in_dim(block, block.shape[dim] - width, None, axis...  24 us
    unnamed x141, local copies, waits for them, and re-layouts  22.9 us
    all_gather x2, blocking collectives, precondition(): everyone = lax.all_gather(restricted, 'wide', axis=0, tiled=True)  17.9 us
    ppermute x12, waiting for transfers between devices, with_halo(): lax.ppermute(lax.slice_in_dim(block, block.shape[dim] - width, None, axis...  17.3 us
    ppermute x12, starting transfers between devices, with_halo(): lax.ppermute(lax.slice_in_dim(block, 0, width, axis=dim), axis, backward)  14.4 us
  transfers between devices with their start and end apart: 24, of which 8 were waited for; matrix products, arithmetic and copies ran while one was open for 5% of the time, Pallas kernels for 0%

profile of v1, /device:TPU:0, one launch (start us, length us, event | category | flops | bytes accessed | tf_op | source)
XLA Modules:
  0.0 343.1 jit_solution(13955799774175822417)
XLA Ops:
  1.8 3.4 collective-permute-start.3
  6.5 5.2 %collective-permute-start = (bf16[1,3,128,128]{3,2,1,0:T(8,128)(2,1)S(1)}, bf16[1,3,128,128]{3,2,1,0:T(8,128)(2,1)}, u32[]{:S(2)}, u32[]{:S(2)}) collective-permute-start(bf16[1,3,128,128]{3,2,1,0:T(8,128)(2,1)S(1)} %get-tuple-element.36), channel_id=1, source_target_pairs={{0,1},{1,2},{2,3},{4,5},{5,6},{6,7},{8,9},{9,10},{10,11},{12,13},{... | collective-permute-start | bytes 294920 | tf_op jit(solution)/shard_map/ppermute | solution.py:17
  23.3 6.6 %fusion.23 = f32[3,1024,128]{1,2,0:T(8,128)} fusion(bf16[1,1,3,1024,1024]{4,3,2,1,0:T(8,128)(2,1)} %param.12, f32[3,1024,128]{1,2,0:T(8,128)S(1)} %copy.76, f32[3,1024,128]{1,2,0:T(8,128)} %copy.77, f32[3,1024]{1,0:T(4,128)S(1)} %copy-done.29, pred[3,1024]{1,0:T(4,128)(4,1)S(1)} %bitcast.430), kind=kOutput, calls=%fused_computation.50 | convolution fusion | flops 807272448 | bytes 11025408 | tf_op jit(solution)/shard_map/sij,sjr->sir/dot_general | solution.py:106
  39.5 4.6 %collective-permute-done.5 = f32[1,3,128,128]{3,2,1,0:T(8,128)S(1)} collective-permute-done((f32[1,3,128,128]{3,2,1,0:T(8,128)S(1)}, f32[1,3,128,128]{3,2,1,0:T(8,128)S(1)}, u32[]{:S(2)}, u32[]{:S(2)}) %collective-permute-start.5) | collective-permute-done | bytes 196640 | tf_op jit(solution)/shard_map/ppermute | solution.py:20
  49.2 14.8 %all-gather = f32[32,128]{1,0:T(8,128)S(1)} all-gather(f32[8,128]{1,0:T(8,128)S(1)} %convolution_bitcast_fusion.1), channel_id=2, replica_groups=mesh['wide'=8,'narrow'=4] {'narrow'}, dimensions={0}, use_global_device_ids=true | all-gather | bytes 20480 | tf_op jit(solution)/shard_map/all_gather | solution.py:126
  64.0 8.1 %all_gather.27 = f32[64,128]{1,0:T(8,128)S(1)} all-gather(f32[8,128]{1,0:T(8,128)S(1)} %bitcast_reduce_fusion.1), channel_id=1, replica_groups=mesh['wide'=8,'narrow'=4] {'wide'}, dimensions={0}, use_global_device_ids=true | all-gather | bytes 36864 | tf_op jit(solution)/shard_map/all_gather | solution.py:128
  72.1 13.1 %all_gather.24 = f32[96,128]{1,0:T(8,128)S(1)} all-gather(f32[24,128]{1,0:T(8,128)S(1)} %bitcast.427), channel_id=1, replica_groups=mesh['wide'=8,'narrow'=4] {'narrow'}, dimensions={0}, use_global_device_ids=true | all-gather | bytes 61440 | tf_op jit(solution)/shard_map/all_gather | solution.py:123
  94.2 4.4 %collective-permute-done.9 = f32[1,3,128,128]{3,2,1,0:T(8,128)S(1)} collective-permute-done((f32[1,3,128,128]{3,2,1,0:T(8,128)S(1)}, f32[1,3,128,128]{3,2,1,0:T(8,128)S(1)}, u32[]{:S(2)}, u32[]{:S(2)}) %collective-permute-start.9) | collective-permute-done | bytes 196640 | tf_op jit(solution)/shard_map/ppermute | solution.py:20
  103.1 3.4 %fusion.26 = f32[3,1024,128]{1,2,0:T(8,128)} fusion(bf16[3,1024,128]{2,1,0:T(8,128)(2,1)S(1)} %bitcast.420, bf16[1,1,3,1024,1024]{4,3,2,1,0:T(8,128)(2,1)S(1)} %bitcast.404), kind=kOutput, calls=%fused_computation.51 | convolution fusion | flops 805306368 | bytes 8650752 | tf_op jit(solution)/shard_map/sij,sjr->sir/dot_general | solution.py:106
  106.6 3.0 copy.96
  113.6 5.4 %collective-permute-start.12 = (f32[1,3,128,128]{3,2,1,0:T(8,128)}, f32[1,3,128,128]{3,2,1,0:T(8,128)}, u32[]{:S(2)}, u32[]{:S(2)}) collective-permute-start(f32[1,3,128,128]{3,2,1,0:T(8,128)} %get-tuple-element.24), channel_id=1, source_target_pairs={{0,1},{1,2},{2,3},{4,5},{5,6},{6,7},{8,9},{9,10},{10,11},{12,13},{... | collective-permute-start | bytes 589832 | tf_op jit(solution)/shard_map/ppermute | solution.py:17
  120.8 41.0 %all-reduce = (f32[128]{0:T(128)S(1)}, f32[128]{0:T(128)S(1)}) all-reduce(f32[128]{0:T(128)S(1)} %get-tuple-element.20, f32[128]{0:T(128)S(1)} %get-tuple-element.8), channel_id=1, replica_groups=mesh['wide'=8,'narrow'=4] {'wide','narrow'}, use_global_device_ids=true, to_apply=%region_5.6 | all-reduce | flops 256 | bytes 2048 | tf_op jit(solution)/shard_map/psum | solution.py:99
  169.8 13.2 %all-gather.1 = f32[32,128]{1,0:T(8,128)S(1)} all-gather(f32[8,128]{1,0:T(8,128)S(1)} %convolution_bitcast_fusion), channel_id=3, replica_groups=mesh['wide'=8,'narrow'=4] {'narrow'}, dimensions={0}, use_global_device_ids=true | all-gather | bytes 20480 | tf_op jit(solution)/shard_map/all_gather | solution.py:126
  183.0 9.9 %all_gather.31 = f32[64,128]{1,0:T(8,128)S(1)} all-gather(f32[8,128]{1,0:T(8,128)S(1)} %bitcast_reduce_fusion), channel_id=1, replica_groups=mesh['wide'=8,'narrow'=4] {'wide'}, dimensions={0}, use_global_device_ids=true | all-gather | bytes 36864 | tf_op jit(solution)/shard_map/all_gather | solution.py:128
  193.2 13.1 %all_gather.28 = f32[96,128]{1,0:T(8,128)S(1)} all-gather(f32[24,128]{1,0:T(8,128)S(1)} %bitcast.426), channel_id=1, replica_groups=mesh['wide'=8,'narrow'=4] {'narrow'}, dimensions={0}, use_global_device_ids=true | all-gather | bytes 61440 | tf_op jit(solution)/shard_map/all_gather | solution.py:123
  206.7 4.4 %multiply_reduce_fusion.1 = (f32[128]{0:T(128)}, f32[3,8,128,128]{3,2,1,0:T(8,128)}) fusion(f32[3,8,128,128]{3,2,1,0:T(8,128)} %copy-done.20, bf16[1,1,3,8,128,128]{5,4,3,2,1,0:T(8,128)(2,1)S(1)} %copy-done.25, f32[3,8,128]{2,1,0:T(8,128)S(1)} %fusion.32, bf16[3,8,128,128]{2,3,1,0:T(8,128)(2,1)S(1)} %get-tuple-element.40, f32[3,8,128]{2,1,0:T(8,128)S(1)} %bitcast.425, ...), kind=kOutput, calls=%fused_computation.39 | convolution fusion | flops 204078976 | bytes 5542400 | tf_op jit(solution)/shard_map/sfjk,sfkr->sfjr/dot_general | solution.py:135
  216.8 40.3 %psum.30 = f32[128]{0:T(128)S(1)} all-reduce(f32[128]{0:T(128)S(1)} %copy-done.38), channel_id=1, replica_groups=mesh['wide'=8,'narrow'=4] {'wide','narrow'}, use_global_device_ids=true, to_apply=%region_13.14 | all-reduce | flops 128 | bytes 1024 | tf_op jit(solution)/shard_map/psum | solution.py:99
  260.1 6.1 %collective-permute-done.18 = f32[1,3,128,128]{3,2,1,0:T(8,128)S(1)} collective-permute-done((f32[1,3,128,128]{3,2,1,0:T(8,128)S(1)}, f32[1,3,128,128]{3,2,1,0:T(8,128)S(1)}, u32[]{:S(2)}, u32[]{:S(2)}) %collective-permute-start.18) | collective-permute-done | bytes 196640 | tf_op jit(solution)/shard_map/ppermute | solution.py:17
  271.1 3.4 fusion.29
  277.6 3.2 multiply_reduce_fusion
  280.8 39.2 %psum.31 = f32[128]{0:T(128)S(1)} all-reduce(f32[128]{0:T(128)S(1)} %get-tuple-element.4), channel_id=1, replica_groups=mesh['wide'=8,'narrow'=4] {'wide','narrow'}, use_global_device_ids=true, to_apply=%region_16.17 | all-reduce | flops 128 | bytes 1024 | tf_op jit(solution)/shard_map/psum | solution.py:99
  322.6 4.6 %collective-permute-start.20 = (f32[1,3,128,128]{3,2,1,0:T(8,128)S(1)}, f32[1,3,128,128]{3,2,1,0:T(8,128)S(1)}, u32[]{:S(2)}, u32[]{:S(2)}) collective-permute-start(f32[1,3,128,128]{3,2,1,0:T(8,128)S(1)} %get-tuple-element.15), channel_id=1, source_target_pairs={{0,1},{1,2},{2,3},{4,5},{5,6},{6,7},{8,9},{9,10},{10,11},{12,13},{... | collective-permute-start | bytes 589832 | tf_op jit(solution)/shard_map/ppermute | solution.py:17
  327.2 3.1 fusion.10
  330.9 7.6 %collective-permute-done.22 = f32[1,3,128,128]{3,2,1,0:T(8,128)S(1)} collective-permute-done((f32[1,3,128,128]{3,2,1,0:T(8,128)S(1)}, f32[1,3,128,128]{3,2,1,0:T(8,128)S(1)}, u32[]{:S(2)}, u32[]{:S(2)}) %collective-permute-start.22) | collective-permute-done | bytes 196640 | tf_op jit(solution)/shard_map/ppermute | solution.py:17
  (234 shorter events, 79.6 us)
Async XLA Ops:
  1.8 18.4 %collective-permute-start.3 = (bf16[1,3,128,128]{3,2,1,0:T(8,128)(2,1)S(1)}, bf16[1,3,128,128]{3,2,1,0:T(8,128)(2,1)}, u32[]{:S(2)}, u32[]{:S(2)}) collective-permute-start(bf16[1,3,128,128]{3,2,1,0:T(8,128)(2,1)S(1)} %get-tuple-element.33), channel_id=1, source_target_pairs={{4,0},{8,4},{12,8},{16,12},{20,16},{24,20},{28,24},{0,28},{5,1},{9... | collective-permute-start | bytes 294920 | tf_op jit(solution)/shard_map/ppermute | solution.py:20
  5.2 14.1 %collective-permute-start.2 = (bf16[1,3,128,128]{3,2,1,0:T(8,128)(2,1)S(1)}, bf16[1,3,128,128]{3,2,1,0:T(8,128)(2,1)}, u32[]{:S(2)}, u32[]{:S(2)}) collective-permute-start(bf16[1,3,128,128]{3,2,1,0:T(8,128)(2,1)S(1)} %get-tuple-element.34), channel_id=1, source_target_pairs={{0,4},{4,8},{8,12},{12,16},{16,20},{20,24},{24,28},{28,0},{1,5},{5... | collective-permute-start | bytes 294920 | tf_op jit(solution)/shard_map/ppermute | solution.py:17
  5.2 13.2 %collective-permute-start.1 = (bf16[1,3,128,128]{3,2,1,0:T(8,128)(2,1)S(1)}, bf16[1,3,128,128]{3,2,1,0:T(8,128)(2,1)}, u32[]{:S(2)}, u32[]{:S(2)}) collective-permute-start(bf16[1,3,128,128]{3,2,1,0:T(8,128)(2,1)S(1)} %get-tuple-element.35), channel_id=1, source_target_pairs={{1,0},{2,1},{3,2},{5,4},{6,5},{7,6},{9,8},{10,9},{11,10},{13,12},{... | collective-permute-start | bytes 294920 | tf_op jit(solution)/shard_map/ppermute | solution.py:20
  6.5 11.0 %collective-permute-start = (bf16[1,3,128,128]{3,2,1,0:T(8,128)(2,1)S(1)}, bf16[1,3,128,128]{3,2,1,0:T(8,128)(2,1)}, u32[]{:S(2)}, u32[]{:S(2)}) collective-permute-start(bf16[1,3,128,128]{3,2,1,0:T(8,128)(2,1)S(1)} %get-tuple-element.36), channel_id=1, source_target_pairs={{0,1},{1,2},{2,3},{4,5},{5,6},{6,7},{8,9},{9,10},{10,11},{12,13},{... | collective-permute-start | bytes 294920 | tf_op jit(solution)/shard_map/ppermute | solution.py:17
  33.1 6.4 %collective-permute-start.4 = (f32[1,3,128,128]{3,2,1,0:T(8,128)S(1)}, f32[1,3,128,128]{3,2,1,0:T(8,128)S(1)}, u32[]{:S(2)}, u32[]{:S(2)}) collective-permute-start(f32[1,3,128,128]{3,2,1,0:T(8,128)S(1)} %get-tuple-element.32), channel_id=1, source_target_pairs={{0,1},{1,2},{2,3},{4,5},{5,6},{6,7},{8,9},{9,10},{10,11},{12,13},{... | collective-permute-start | bytes 589832 | tf_op jit(solution)/shard_map/ppermute | solution.py:17
  35.9 8.1 %collective-permute-start.5 = (f32[1,3,128,128]{3,2,1,0:T(8,128)S(1)}, f32[1,3,128,128]{3,2,1,0:T(8,128)S(1)}, u32[]{:S(2)}, u32[]{:S(2)}) collective-permute-start(f32[1,3,128,128]{3,2,1,0:T(8,128)S(1)} %get-tuple-element.31), channel_id=1, source_target_pairs={{1,0},{2,1},{3,2},{5,4},{6,5},{7,6},{9,8},{10,9},{11,10},{13,12},{... | collective-permute-start | bytes 589832 | tf_op jit(solution)/shard_map/ppermute | solution.py:20
  37.2 7.9 %collective-permute-start.7 = (f32[1,3,128,128]{3,2,1,0:T(8,128)S(1)}, f32[1,3,128,128]{3,2,1,0:T(8,128)S(1)}, u32[]{:S(2)}, u32[]{:S(2)}) collective-permute-start(f32[1,3,128,128]{3,2,1,0:T(8,128)S(1)} %get-tuple-element.29), channel_id=1, source_target_pairs={{4,0},{8,4},{12,8},{16,12},{20,16},{24,20},{28,24},{0,28},{5,1},{9... | collective-permute-start | bytes 589832 | tf_op jit(solution)/shard_map/ppermute | solution.py:20
  39.1 6.0 %collective-permute-start.6 = (f32[1,3,128,128]{3,2,1,0:T(8,128)S(1)}, f32[1,3,128,128]{3,2,1,0:T(8,128)S(1)}, u32[]{:S(2)}, u32[]{:S(2)}) collective-permute-start(f32[1,3,128,128]{3,2,1,0:T(8,128)S(1)} %get-tuple-element.30), channel_id=1, source_target_pairs={{0,4},{4,8},{8,12},{12,16},{16,20},{20,24},{24,28},{28,0},{1,5},{5... | collective-permute-start | bytes 589832 | tf_op jit(solution)/shard_map/ppermute | solution.py:17
  88.5 5.7 %collective-permute-start.8 = (f32[1,3,128,128]{3,2,1,0:T(8,128)S(1)}, f32[1,3,128,128]{3,2,1,0:T(8,128)S(1)}, u32[]{:S(2)}, u32[]{:S(2)}) collective-permute-start(f32[1,3,128,128]{3,2,1,0:T(8,128)S(1)} %get-tuple-element.28), channel_id=1, source_target_pairs={{0,1},{1,2},{2,3},{4,5},{5,6},{6,7},{8,9},{9,10},{10,11},{12,13},{... | collective-permute-start | bytes 589832 | tf_op jit(solution)/shard_map/ppermute | solution.py:17
  91.0 7.6 %collective-permute-start.9 = (f32[1,3,128,128]{3,2,1,0:T(8,128)S(1)}, f32[1,3,128,128]{3,2,1,0:T(8,128)S(1)}, u32[]{:S(2)}, u32[]{:S(2)}) collective-permute-start(f32[1,3,128,128]{3,2,1,0:T(8,128)S(1)} %get-tuple-element.27), channel_id=1, source_target_pairs={{1,0},{2,1},{3,2},{5,4},{6,5},{7,6},{9,8},{10,9},{11,10},{13,12},{... | collective-permute-start | bytes 589832 | tf_op jit(solution)/shard_map/ppermute | solution.py:20
  92.3 7.3 %collective-permute-start.11 = (f32[1,3,128,128]{3,2,1,0:T(8,128)S(1)}, f32[1,3,128,128]{3,2,1,0:T(8,128)S(1)}, u32[]{:S(2)}, u32[]{:S(2)}) collective-permute-start(f32[1,3,128,128]{3,2,1,0:T(8,128)S(1)} %get-tuple-element.25), channel_id=1, source_target_pairs={{4,0},{8,4},{12,8},{16,12},{20,16},{24,20},{28,24},{0,28},{5,1},{9... | collective-permute-start | bytes 589832 | tf_op jit(solution)/shard_map/ppermute | solution.py:20
  92.3 7.2 %collective-permute-start.10 = (f32[1,3,128,128]{3,2,1,0:T(8,128)S(1)}, f32[1,3,128,128]{3,2,1,0:T(8,128)S(1)}, u32[]{:S(2)}, u32[]{:S(2)}) collective-permute-start(f32[1,3,128,128]{3,2,1,0:T(8,128)S(1)} %get-tuple-element.26), channel_id=1, source_target_pairs={{0,4},{4,8},{8,12},{12,16},{16,20},{20,24},{24,28},{28,0},{1,5},{5... | collective-permute-start | bytes 589832 | tf_op jit(solution)/shard_map/ppermute | solution.py:17
  113.6 48.3 %collective-permute-start.12 = (f32[1,3,128,128]{3,2,1,0:T(8,128)}, f32[1,3,128,128]{3,2,1,0:T(8,128)}, u32[]{:S(2)}, u32[]{:S(2)}) collective-permute-start(f32[1,3,128,128]{3,2,1,0:T(8,128)} %get-tuple-element.24), channel_id=1, source_target_pairs={{0,1},{1,2},{2,3},{4,5},{5,6},{6,7},{8,9},{9,10},{10,11},{12,13},{... | collective-permute-start | bytes 589832 | tf_op jit(solution)/shard_map/ppermute | solution.py:17
  118.9 43.9 %collective-permute-start.13 = (f32[1,3,128,128]{3,2,1,0:T(8,128)}, f32[1,3,128,128]{3,2,1,0:T(8,128)}, u32[]{:S(2)}, u32[]{:S(2)}) collective-permute-start(f32[1,3,128,128]{3,2,1,0:T(8,128)} %get-tuple-element.23), channel_id=1, source_target_pairs={{1,0},{2,1},{3,2},{5,4},{6,5},{7,6},{9,8},{10,9},{11,10},{13,12},{... | collective-permute-start | bytes 589832 | tf_op jit(solution)/shard_map/ppermute | solution.py:20
  120.2 44.5 %collective-permute-start.15 = (f32[1,3,128,128]{3,2,1,0:T(8,128)S(1)}, f32[1,3,128,128]{3,2,1,0:T(8,128)}, u32[]{:S(2)}, u32[]{:S(2)}) collective-permute-start(f32[1,3,128,128]{3,2,1,0:T(8,128)S(1)} %get-tuple-element.21), channel_id=1, source_target_pairs={{4,0},{8,4},{12,8},{16,12},{20,16},{24,20},{28,24},{0,28},{5,1},{9... | collective-permute-start | bytes 589832 | tf_op jit(solution)/shard_map/ppermute | solution.py:20
  120.3 43.5 %collective-permute-start.14 = (f32[1,3,128,128]{3,2,1,0:T(8,128)}, f32[1,3,128,128]{3,2,1,0:T(8,128)}, u32[]{:S(2)}, u32[]{:S(2)}) collective-permute-start(f32[1,3,128,128]{3,2,1,0:T(8,128)} %get-tuple-element.22), channel_id=1, source_target_pairs={{0,4},{4,8},{8,12},{12,16},{16,20},{20,24},{24,28},{28,0},{1,5},{5... | collective-permute-start | bytes 589832 | tf_op jit(solution)/shard_map/ppermute | solution.py:17
  213.2 45.0 %collective-permute-start.16 = (f32[1,3,128,128]{3,2,1,0:T(8,128)}, f32[1,3,128,128]{3,2,1,0:T(8,128)}, u32[]{:S(2)}, u32[]{:S(2)}) collective-permute-start(f32[1,3,128,128]{3,2,1,0:T(8,128)} %get-tuple-element.19), channel_id=1, source_target_pairs={{0,1},{1,2},{2,3},{4,5},{5,6},{6,7},{8,9},{9,10},{10,11},{12,13},{... | collective-permute-start | bytes 589832 | tf_op jit(solution)/shard_map/ppermute | solution.py:17
  215.5 43.6 %collective-permute-start.17 = (f32[1,3,128,128]{3,2,1,0:T(8,128)S(1)}, f32[1,3,128,128]{3,2,1,0:T(8,128)}, u32[]{:S(2)}, u32[]{:S(2)}) collective-permute-start(f32[1,3,128,128]{3,2,1,0:T(8,128)S(1)} %get-tuple-element.18), channel_id=1, source_target_pairs={{1,0},{2,1},{3,2},{5,4},{6,5},{7,6},{9,8},{10,9},{11,10},{13,12},{... | collective-permute-start | bytes 589832 | tf_op jit(solution)/shard_map/ppermute | solution.py:20
  257.2 9.0 %collective-permute-start.19 = (f32[1,3,128,128]{3,2,1,0:T(8,128)S(1)}, f32[1,3,128,128]{3,2,1,0:T(8,128)S(1)}, u32[]{:S(2)}, u32[]{:S(2)}) collective-permute-start(f32[1,3,128,128]{3,2,1,0:T(8,128)S(1)} %get-tuple-element.16), channel_id=1, source_target_pairs={{4,0},{8,4},{12,8},{16,12},{20,16},{24,20},{28,24},{0,28},{5,1},{9... | collective-permute-start | bytes 589832 | tf_op jit(solution)/shard_map/ppermute | solution.py:20
  258.1 8.0 %collective-permute-start.18 = (f32[1,3,128,128]{3,2,1,0:T(8,128)S(1)}, f32[1,3,128,128]{3,2,1,0:T(8,128)S(1)}, u32[]{:S(2)}, u32[]{:S(2)}) collective-permute-start(f32[1,3,128,128]{3,2,1,0:T(8,128)S(1)} %get-tuple-element.17), channel_id=1, source_target_pairs={{0,4},{4,8},{8,12},{12,16},{16,20},{20,24},{24,28},{28,0},{1,5},{5... | collective-permute-start | bytes 589832 | tf_op jit(solution)/shard_map/ppermute | solution.py:17
  321.3 9.6 %collective-permute-start.21 = (f32[1,3,128,128]{3,2,1,0:T(8,128)S(1)}, f32[1,3,128,128]{3,2,1,0:T(8,128)S(1)}, u32[]{:S(2)}, u32[]{:S(2)}) collective-permute-start(f32[1,3,128,128]{3,2,1,0:T(8,128)S(1)} %get-tuple-element.14), channel_id=1, source_target_pairs={{1,0},{2,1},{3,2},{5,4},{6,5},{7,6},{9,8},{10,9},{11,10},{13,12},{... | collective-permute-start | bytes 589832 | tf_op jit(solution)/shard_map/ppermute | solution.py:20
  322.6 8.3 %collective-permute-start.20 = (f32[1,3,128,128]{3,2,1,0:T(8,128)S(1)}, f32[1,3,128,128]{3,2,1,0:T(8,128)S(1)}, u32[]{:S(2)}, u32[]{:S(2)}) collective-permute-start(f32[1,3,128,128]{3,2,1,0:T(8,128)S(1)} %get-tuple-element.15), channel_id=1, source_target_pairs={{0,1},{1,2},{2,3},{4,5},{5,6},{6,7},{8,9},{9,10},{10,11},{12,13},{... | collective-permute-start | bytes 589832 | tf_op jit(solution)/shard_map/ppermute | solution.py:17
  330.3 8.1 %collective-permute-start.23 = (f32[1,3,128,128]{3,2,1,0:T(8,128)S(1)}, f32[1,3,128,128]{3,2,1,0:T(8,128)S(1)}, u32[]{:S(2)}, u32[]{:S(2)}) collective-permute-start(f32[1,3,128,128]{3,2,1,0:T(8,128)S(1)} %get-tuple-element.12), channel_id=1, source_target_pairs={{4,0},{8,4},{12,8},{16,12},{20,16},{24,20},{28,24},{0,28},{5,1},{9... | collective-permute-start | bytes 589832 | tf_op jit(solution)/shard_map/ppermute | solution.py:20
  330.7 7.8 %collective-permute-start.22 = (f32[1,3,128,128]{3,2,1,0:T(8,128)S(1)}, f32[1,3,128,128]{3,2,1,0:T(8,128)S(1)}, u32[]{:S(2)}, u32[]{:S(2)}) collective-permute-start(f32[1,3,128,128]{3,2,1,0:T(8,128)S(1)} %get-tuple-element.13), channel_id=1, source_target_pairs={{0,4},{4,8},{8,12},{12,16},{16,20},{20,24},{24,28},{28,0},{1,5},{5... | collective-permute-start | bytes 589832 | tf_op jit(solution)/shard_map/ppermute | solution.py:17
  (47 other events, 707.3 us)
